TPU v7x, 512 devices: a whole 4x8x8 slice. The times are simulated.
512 devices in a mesh: dom: 64 (over x, y, core), mem: 8 (over z).
Axes of the slice: x: 4, y: 8, z: 8, core: 2. Of those that a mesh axis runs over, the one named last changes fastest.
Arguments:
- ensemble: bfloat16 [48, 32, 262144], P('mem', None, 'dom'), may hold values from -6 to 6
- observed: float32 [32, 65536], P(None, 'dom'), may hold values from -6 to 6
- tile_weight: bfloat16 [6144, 128, 128], P('dom')
- tile_block: int32 [6144], P('dom'), may hold values from 0 to 31
- tile_target: int32 [6144], P('dom'), may hold values from 0 to 511, as said below
- tile_count: int32 [64], P('dom'), may hold values from 48 to 96, as said below
Outputs:
- crps: float32 [32, 65536], P(None, 'dom')
Inputs may be any that keep to these rules, and one draw needn't show every extreme that they name: `tile_block`: a slot's source block, counted within its partition's cells. `tile_target`: slot k belongs to partition p = k // 96; its target tile is owned by one of the partitions p - 4 to p + 4, where partition o owns the 8 target tiles from o * 8 on. The live slots of partition p are the first tile_count[p] of its list; the rest are padding.
All inputs are finite; a program needn't handle non-finite values.
Results may differ from a plain program's by a relative error of at most 0.0003.
Values sent between devices are 32-bit elements; how exact they have to be, the bound alone decides.
No kernel may reach another device: no remote copies, remote signals or barrier semaphores. Data moves between devices by JAX's collectives and lax.ppermute only.
A program may use at most 64 MiB of HBM per device.

v0:
```python
import math
import jax
import jax.numpy as jnp
from jax import lax
from jax.sharding import PartitionSpec as P

REACH = 4


def from_behind(value, axis, steps):
    count = lax.axis_size(axis)
    first, last = (max(0, -steps), min(count, count - steps))
    return lax.ppermute(value, axis, [(source, source + steps) for source in range(first, last)])


def sent_to_all(shard, axis):
    copies = jnp.broadcast_to(shard, (lax.axis_size(axis), *shard.shape))
    return lax.all_to_all(copies, axis, split_axis=0, concat_axis=0, tiled=True)


def laid_out(pieces, dim):
    pieces = jnp.moveaxis(pieces, 0, dim)
    lengths = pieces.shape
    return pieces.reshape(*lengths[:dim], lengths[dim] * lengths[dim + 1], *lengths[dim + 2 :])


def gathered_copies(shard, axis, dim):
    pieces = sent_to_all(shard, axis)
    return laid_out(pieces, dim)


def pair_total(left_set, right_set):
    flat_left = left_set.reshape(left_set.shape[0], -1)
    flat_right = right_set.reshape(right_set.shape[0], -1)
    total_columns = flat_left.shape[1]
    block_span = math.gcd(total_columns, 1024)

    def block_pairs(first_column):
        left_cols = lax.dynamic_slice_in_dim(flat_left, first_column, block_span, 1)
        right_cols = lax.dynamic_slice_in_dim(flat_right, first_column, block_span, 1)
        return jnp.sum(jnp.abs(left_cols[:, None, :] - right_cols[None, :, :]), axis=(0, 1))

    column_starts = jnp.arange(total_columns // block_span, dtype=jnp.int32) * block_span
    return lax.map(block_pairs, column_starts).reshape(left_set.shape[1:])


def on_device(ensemble, observed, tile_weight, tile_block, tile_target, tile_count):
    groups, levels, src_cells = ensemble.shape
    block_cells = tile_weight.shape[1]
    channels = groups * levels
    tile_slots = tile_block.shape[0]
    values = ensemble.reshape(channels, src_cells // block_cells, block_cells)
    picked = jnp.take(values, tile_block, axis=1)
    partial_value = jnp.einsum(
        "csi,sij->scj", picked, tile_weight, preferred_element_type=jnp.float32
    )
    owned = observed.shape[1] // block_cells
    window = 2 * REACH + 1
    device = lax.axis_index("dom")
    local_tile = tile_target - (device - REACH) * owned
    rows_index = jnp.arange(window * owned, dtype=jnp.int32)
    is_live = jnp.arange(tile_slots, dtype=jnp.int32) < tile_count[0]
    chooser = ((rows_index[:, None] == local_tile[None, :]) & is_live[None, :]).astype(jnp.float32)
    owner_parts = jnp.dot(
        chooser,
        partial_value.reshape(tile_slots, channels * block_cells),
        precision=lax.Precision.HIGHEST,
        preferred_element_type=jnp.float32,
    )
    owner_parts = owner_parts.reshape(window, owned, channels * block_cells)
    summed = owner_parts[REACH]
    pending = {}
    for offset in range(1, REACH + 1):
        pending[1, offset] = owner_parts[REACH + offset]
        pending[-1, offset] = owner_parts[REACH - offset]
    for level_bit in range(REACH.bit_length()):
        stride = 1 << level_bit
        for heading in (1, -1):
            moving = [
                offset
                for offset in range(1, REACH + 1)
                if (heading, offset) in pending and offset & stride
            ]
            if moving:
                outgoing = jnp.stack([pending.pop((heading, offset)) for offset in moving])
                incoming = from_behind(outgoing, "dom", heading * stride)
                for position, offset in enumerate(moving):
                    landing = offset - stride
                    if landing == 0:
                        summed = summed + incoming[position]
                    else:
                        pending[heading, landing] = pending[heading, landing] + incoming[position]
    remapped = (
        summed.reshape(owned, groups, levels, block_cells)
        .transpose(1, 2, 0, 3)
        .reshape(groups, levels, owned * block_cells)
    )
    members = groups * lax.axis_size("mem")
    norm_pairs = 2.0 * members * (members - 1)
    regrouped = lax.all_to_all(remapped, "mem", split_axis=2, concat_axis=0, tiled=True)
    part_cells = regrouped.shape[2]
    observed_part = lax.dynamic_slice_in_dim(
        observed, lax.axis_index("mem") * part_cells, part_cells, 1
    )
    skill_sum = jnp.sum(jnp.abs(regrouped - observed_part[None]), axis=0)
    spread = pair_total(regrouped, regrouped)
    score_part = skill_sum / members - spread / norm_pairs
    return gathered_copies(score_part, "mem", 1)


def solution(mesh):
    return jax.shard_map(
        on_device,
        mesh=mesh,
        in_specs=(
            P("mem", None, "dom"),
            P(None, "dom"),
            P("dom", None, None),
            P("dom"),
            P("dom"),
            P("dom"),
        ),
        out_specs=P(None, "dom"),
        check_vma=False,
    )
```

profile of v0, /device:TPU:2, one launch (start us, length us, event | category | flops | bytes accessed | tf_op | source)
XLA Modules:
  0.0 198.6 jit_solution(17366331627590352062)
XLA Ops:
  0.0 0.0 copy-start
  0.0 0.0 copy-start.1
  0.0 0.8 compare_select_fusion
  0.8 0.8 compare_and_fusion
  1.6 1.7 copy.26
  3.4 1.8 copy.18
  5.8 0.0 copy-done.1
  5.9 4.8 %gather_fusion = bf16[96,192,128]{2,1,0:T(8,128)(2,1)} fusion(bf16[192,32,128]{2,0,1:T(8,128)(2,1)} %copy.18, s32[1024]{0:T(1024)S(1)} %pad_clamp_fusion), kind=kCustom, calls=%fused_computation | custom fusion | bytes 9437568 | tf_op jit(solution)/shard_map/jit(_take)/gather | solution.py:53
  10.7 0.0 copy-done
  10.7 3.4 %fusion.3 = f32[96,192,128]{2,1,0:T(8,128)S(1)} fusion(bf16[96,128,128]{2,1,0:T(8,128)(2,1)S(1)} %copy-done, bf16[96,192,128]{2,1,0:T(8,128)(2,1)} %gather_fusion, pred[96]{0:T(512)(128)(4,1)S(1)} %compare_and_fusion), kind=kOutput, calls=%fused_computation.6 | convolution fusion | flops 606339072 | bytes 17301600 | tf_op jit(solution)/shard_map/csi,sij->scj/dot_general | solution.py:54
  14.1 10.0 %fusion = f32[72,24576]{1,0:T(8,128)S(1)} fusion(f32[12,8,192,128]{3,2,1,0:T(8,128)S(1)} %bitcast.71, s32[96]{0:T(128)S(1)} %broadcast_subtract_fusion, pred[96]{0:T(512)(128)(4,1)S(1)} %iota_compare_fusion.1), kind=kOutput, calls=%fused_computation.3 | convolution fusion | flops 2038445568 | bytes 16515552 | tf_op jit(solution)/shard_map/dot_general | solution.py:64
  24.1 0.4 fusion.15
  24.5 0.1 pad_maximum_fusion.1
  24.6 4.8 %collective-permute-start.1 = (f32[2,8,24576]{2,1,0:T(8,128)S(1)}, f32[2,8,24576]{2,1,0:T(8,128)S(1)}, u32[]{:S(2)}, u32[]{:S(2)}) collective-permute-start(f32[2,8,24576]{2,1,0:T(8,128)S(1)} %pad_maximum_fusion.1), channel_id=1, source_target_pairs={{8,0},{16,8},{24,16},{32,24},{40,32},{48,40},{56,48},{64,56},{72,6... | collective-permute-start | bytes 4718600 | tf_op jit(solution)/shard_map/ppermute | solution.py:13
  29.4 0.1 pad_maximum_fusion
  29.5 1.9 collective-permute-start
  31.4 2.1 %collective-permute-start.4 = (f32[1,8,24576]{2,1,0:T(8,128)S(1)}, f32[1,8,24576]{2,1,0:T(8,128)S(1)}, u32[]{:S(2)}, u32[]{:S(2)}) collective-permute-start(f32[1,8,24576]{2,1,0:T(8,128)S(1)} %get-tuple-element.52), channel_id=1, source_target_pairs={{0,32},{8,40},{16,48},{24,56},{32,64},{40,72},{48,80},{56,88},{64,... | collective-permute-start | bytes 2359304 | tf_op jit(solution)/shard_map/ppermute | solution.py:13
  33.6 6.9 %collective-permute-start.5 = (f32[1,8,24576]{2,1,0:T(8,128)S(1)}, f32[1,8,24576]{2,1,0:T(8,128)S(1)}, u32[]{:S(2)}, u32[]{:S(2)}) collective-permute-start(f32[1,8,24576]{2,1,0:T(8,128)S(1)} %get-tuple-element.51), channel_id=1, source_target_pairs={{32,0},{40,8},{48,16},{56,24},{64,32},{72,40},{80,48},{88,56},{96,... | collective-permute-start | bytes 2359304 | tf_op jit(solution)/shard_map/ppermute | solution.py:13
  40.5 28.0 %collective-permute-done.1 = f32[2,8,24576]{2,1,0:T(8,128)S(1)} collective-permute-done((f32[2,8,24576]{2,1,0:T(8,128)S(1)}, f32[2,8,24576]{2,1,0:T(8,128)S(1)}, u32[]{:S(2)}, u32[]{:S(2)}) %collective-permute-start.1) | collective-permute-done | bytes 1572896 | tf_op jit(solution)/shard_map/ppermute | solution.py:13
  68.5 3.9 %collective-permute-done = f32[2,8,24576]{2,1,0:T(8,128)S(1)} collective-permute-done((f32[2,8,24576]{2,1,0:T(8,128)S(1)}, f32[2,8,24576]{2,1,0:T(8,128)S(1)}, u32[]{:S(2)}, u32[]{:S(2)}) %collective-permute-start) | collective-permute-done | bytes 1572896 | tf_op jit(solution)/shard_map/ppermute | solution.py:13
  72.4 0.3 slice_add_fusion.1
  72.6 1.9 collective-permute-start.2
  74.6 6.0 %collective-permute-start.3 = (f32[1,8,24576]{2,1,0:T(8,128)S(1)}, f32[1,8,24576]{2,1,0:T(8,128)S(1)}, u32[]{:S(2)}, u32[]{:S(2)}) collective-permute-start(f32[1,8,24576]{2,1,0:T(8,128)S(1)} %get-tuple-element.58), channel_id=1, source_target_pairs={{16,0},{24,8},{32,16},{40,24},{48,32},{56,40},{64,48},{72,56},{80,... | collective-permute-start | bytes 2359304 | tf_op jit(solution)/shard_map/ppermute | solution.py:13
  80.6 0.0 collective-permute-done.4
  80.6 1.7 collective-permute-done.5
  82.4 18.5 %collective-permute-done.2 = f32[1,8,24576]{2,1,0:T(8,128)S(1)} collective-permute-done((f32[1,8,24576]{2,1,0:T(8,128)S(1)}, f32[1,8,24576]{2,1,0:T(8,128)S(1)}, u32[]{:S(2)}, u32[]{:S(2)}) %collective-permute-start.2) | collective-permute-done | bytes 786464 | tf_op jit(solution)/shard_map/ppermute | solution.py:13
  100.9 0.0 collective-permute-done.3
  100.9 1.2 add_bitcast_fusion
  102.1 4.2 %copy.19 = f32[6,32,8,128]{1,0,3,2:T(8,128)} copy(f32[6,32,8,128]{3,2,1,0:T(8,128)} %add_bitcast_fusion) | data formatting | bytes 1572864 | tf_op jit(solution)/shard_map/transpose | solution.py:95
  106.3 4.6 %reshape.70 = f32[8,1,24576]{2,1,0:T(1,128)} reshape(f32[1024,6,32]{2,1,0:T(8,128)} %bitcast.74) | data formatting | bytes 1572864
  110.9 12.8 %all-to-all-start = ((f32[8,1,24576]{2,1,0:T(1,128)}), f32[8,1,24576]{2,1,0:T(1,128)}, u32[]{:S(2)}, u32[]{:S(2)}) async-start(f32[8,1,24576]{2,1,0:T(1,128)} %reshape.70), calls=%async_computation | async-start | bytes 1572864 | tf_op jit(solution)/shard_map/all_to_all | solution.py:100
  123.7 0.7 constant_dynamic-slice_fusion.1
  124.4 23.2 %all-to-all-done = f32[8,1,24576]{2,1,0:T(1,128)} async-done(((f32[8,1,24576]{2,1,0:T(1,128)}), f32[8,1,24576]{2,1,0:T(1,128)}, u32[]{:S(2)}, u32[]{:S(2)}) %all-to-all-start) | async-done | bytes 786464 | tf_op jit(solution)/shard_map/all_to_all | solution.py:100
  147.6 0.6 broadcast.36
  148.1 4.5 %reduce.1 = f32[8,24576]{1,0:T(8,128)} reduce(f32[8,1,24576]{2,1,0:T(1,128)} %all-to-all-done, f32[]{:T(128)} %broadcast.36), dimensions={1}, to_apply=%all_to_all.14.reduce_sub_computation | reduce | bytes 1572868 | tf_op jit(solution)/shard_map/all_to_all | solution.py:100
  152.6 4.5 %reshape.71 = f32[1024,6,32]{2,1,0:T(8,128)} reshape(f32[8,24576]{1,0:T(8,128)} %reduce.1) | data formatting | bytes 1572864
  157.1 3.4 %copy.21 = f32[8,6,32,128]{3,2,1,0:T(8,128)} copy(f32[8,6,32,128]{2,1,3,0:T(8,128)} %bitcast.72) | data formatting | bytes 1572864 | tf_op jit(solution)/shard_map/all_to_all | solution.py:100
  160.6 2.5 %copy.35 = f32[6,8,32,128]{3,1,2,0:T(8,128)} copy(f32[6,8,32,128]{3,2,1,0:T(8,128)} %bitcast.77) | data formatting | bytes 1572864
  163.0 17.7 %while.11 = (s32[]{:T(128)}, f32[4,1024]{1,0:T(4,128)S(1)}, s32[4]{0:T(128)S(1)}, f32[48,4096]{1,0:T(8,128)}, s32[]{:T(128)}, /*index=5*/s32[]{:T(128)}, s32[]{:T(128)}) while((s32[]{:T(128)}, f32[4,1024]{1,0:T(4,128)S(1)}, s32[4]{0:T(128)S(1)}, f32[48,4096]{1,0:T(8,128)}, s32[]{:T(128)}, /*index=5*/s32[]{:T(128)}, s32[]{:T(128)}) %tuple.33), condition=%wide.region_3.4_spmd, body=%wide.region_1.3_spmd.sunk | while | flops 7076869 | bytes 602243 | solution.py:44
  163.0 0.6 dynamic_slice.20
  165.2 1.1 constant_dynamic-slice_fusion.3
  166.3 1.1 abs_reduce_fusion.2
  167.4 0.1 dynamic_update_slice.6
  167.5 0.6 dynamic_slice.20
  169.7 1.1 constant_dynamic-slice_fusion.3
  170.7 1.1 abs_reduce_fusion.2
  171.8 0.1 dynamic_update_slice.6
  171.9 0.6 dynamic_slice.20
  174.1 1.1 constant_dynamic-slice_fusion.3
  175.1 1.1 abs_reduce_fusion.2
  176.2 0.1 dynamic_update_slice.6
  176.3 0.6 dynamic_slice.20
  178.5 1.0 constant_dynamic-slice_fusion.3
  179.6 1.1 abs_reduce_fusion.2
  180.6 0.1 dynamic_update_slice.6
  180.7 3.9 %copy.23 = f32[6,32,8,128]{3,2,1,0:T(8,128)} copy(f32[6,32,8,128]{1,0,3,2:T(8,128)} %bitcast.73) | data formatting | bytes 1572864 | tf_op jit(solution)/shard_map/all_to_all | solution.py:100
  184.7 1.2 fusion.9
  186.0 11.9 %all_to_all.20 = f32[8,32,128]{2,1,0:T(8,128)S(1)} all-to-all(f32[8,32,128]{2,1,0:T(8,128)S(1)} %broadcast_in_dim.35), channel_id=1, replica_groups=mesh['dom'=64,'mem'=8] {'mem'}, dimensions={0} | all-to-all | bytes 262144 | tf_op jit(solution)/shard_map/all_to_all | solution.py:18
  197.9 0.7 copy_bitcast_fusion.1
  (9 shorter events, 0.1 us)
Async XLA Ops:
  0.0 10.7 %copy-start = (bf16[96,128,128]{2,1,0:T(8,128)(2,1)S(1)}, bf16[96,128,128]{2,1,0:T(8,128)(2,1)}, u32[]{:S(2)}) copy-start(bf16[96,128,128]{2,1,0:T(8,128)(2,1)} %param.10) | copy-start | bytes 9437188
  0.0 5.8 %copy-start.1 = (s32[96]{0:T(128)S(1)}, s32[96]{0:T(128)}, u32[]{:S(2)}) copy-start(s32[96]{0:T(128)} %param.12) | copy-start | bytes 1156
  24.6 43.9 %collective-permute-start.1 = (f32[2,8,24576]{2,1,0:T(8,128)S(1)}, f32[2,8,24576]{2,1,0:T(8,128)S(1)}, u32[]{:S(2)}, u32[]{:S(2)}) collective-permute-start(f32[2,8,24576]{2,1,0:T(8,128)S(1)} %pad_maximum_fusion.1), channel_id=1, source_target_pairs={{8,0},{16,8},{24,16},{32,24},{40,32},{48,40},{56,48},{64,56},{72,6... | collective-permute-start | bytes 4718600 | tf_op jit(solution)/shard_map/ppermute | solution.py:13
  29.5 42.9 %collective-permute-start = (f32[2,8,24576]{2,1,0:T(8,128)S(1)}, f32[2,8,24576]{2,1,0:T(8,128)S(1)}, u32[]{:S(2)}, u32[]{:S(2)}) collective-permute-start(f32[2,8,24576]{2,1,0:T(8,128)S(1)} %pad_maximum_fusion), channel_id=1, source_target_pairs={{0,8},{8,16},{16,24},{24,32},{32,40},{40,48},{48,56},{56,64},{64,7... | collective-permute-start | bytes 4718600 | tf_op jit(solution)/shard_map/ppermute | solution.py:13
  31.4 49.2 %collective-permute-start.4 = (f32[1,8,24576]{2,1,0:T(8,128)S(1)}, f32[1,8,24576]{2,1,0:T(8,128)S(1)}, u32[]{:S(2)}, u32[]{:S(2)}) collective-permute-start(f32[1,8,24576]{2,1,0:T(8,128)S(1)} %get-tuple-element.52), channel_id=1, source_target_pairs={{0,32},{8,40},{16,48},{24,56},{32,64},{40,72},{48,80},{56,88},{64,... | collective-permute-start | bytes 2359304 | tf_op jit(solution)/shard_map/ppermute | solution.py:13
  33.6 48.8 %collective-permute-start.5 = (f32[1,8,24576]{2,1,0:T(8,128)S(1)}, f32[1,8,24576]{2,1,0:T(8,128)S(1)}, u32[]{:S(2)}, u32[]{:S(2)}) collective-permute-start(f32[1,8,24576]{2,1,0:T(8,128)S(1)} %get-tuple-element.51), channel_id=1, source_target_pairs={{32,0},{40,8},{48,16},{56,24},{64,32},{72,40},{80,48},{88,56},{96,... | collective-permute-start | bytes 2359304 | tf_op jit(solution)/shard_map/ppermute | solution.py:13
  72.6 28.2 %collective-permute-start.2 = (f32[1,8,24576]{2,1,0:T(8,128)S(1)}, f32[1,8,24576]{2,1,0:T(8,128)S(1)}, u32[]{:S(2)}, u32[]{:S(2)}) collective-permute-start(f32[1,8,24576]{2,1,0:T(8,128)S(1)} %get-tuple-element.57), channel_id=1, source_target_pairs={{0,16},{8,24},{16,32},{24,40},{32,48},{40,56},{48,64},{56,72},{64,... | collective-permute-start | bytes 2359304 | tf_op jit(solution)/shard_map/ppermute | solution.py:13
  74.6 26.3 %collective-permute-start.3 = (f32[1,8,24576]{2,1,0:T(8,128)S(1)}, f32[1,8,24576]{2,1,0:T(8,128)S(1)}, u32[]{:S(2)}, u32[]{:S(2)}) collective-permute-start(f32[1,8,24576]{2,1,0:T(8,128)S(1)} %get-tuple-element.58), channel_id=1, source_target_pairs={{16,0},{24,8},{32,16},{40,24},{48,32},{56,40},{64,48},{72,56},{80,... | collective-permute-start | bytes 2359304 | tf_op jit(solution)/shard_map/ppermute | solution.py:13
  110.9 36.7 %all-to-all-start = ((f32[8,1,24576]{2,1,0:T(1,128)}), f32[8,1,24576]{2,1,0:T(1,128)}, u32[]{:S(2)}, u32[]{:S(2)}) async-start(f32[8,1,24576]{2,1,0:T(1,128)} %reshape.70), calls=%async_computation | async-start | bytes 1572864 | tf_op jit(solution)/shard_map/all_to_all | solution.py:100
where the time goes:
time: 200 us; the launch traced here: 199 us
  waiting for transfers between devices  75.3 us (38%)
  local copies, waits for them, and re-layouts  40.5 us (20%)
  starting transfers between devices  36.5 us (18%)
  other arithmetic  13.4 us (7%)
  matrix products  13.4 us (7%)
  blocking collectives  11.9 us (6%)
  loops' own time  6.69 us (3%)
    ppermute x6, waiting for transfers between devices, from_behind(): lax.ppermute(value, axis, [(source, source + steps) for source in range(f...  52.1 us
    ppermute x6, starting transfers between devices, from_behind(): lax.ppermute(value, axis, [(source, source + steps) for source in range(f...  23.7 us
    all_to_all x1, waiting for transfers between devices, on_device(): lax.all_to_all(remapped, 'mem', split_axis=2, concat_axis=0, tiled=True)  23.2 us
    unnamed x8, local copies, waits for them, and re-layouts  13.3 us
    all_to_all x1, starting transfers between devices, on_device(): lax.all_to_all(remapped, 'mem', split_axis=2, concat_axis=0, tiled=True)  12.8 us
    all_to_all x1, blocking collectives, sent_to_all(): return lax.all_to_all(copies, axis, split_axis=0, concat_axis=0, tiled=True)  11.9 us
    dot_general x1, matrix products, on_device(): jnp.dot(chooser, partial_value.reshape(tile_slots, channels * block_cells...  10 us
    all_to_all x3, local copies, waits for them, and re-layouts, on_device(): lax.all_to_all(remapped, 'mem', split_axis=2, concat_axis=0, tiled=True)  7.94 us
  transfers between devices with their start and end apart: 7, of which 5 were waited for; matrix products, arithmetic and copies ran while one was open for 1% of the time, Pallas kernels for 0%

commit v1 on v0

--- a/solution.py
+++ b/solution.py
@@ -97,7 +97,9 @@
     )
     members = groups * lax.axis_size("mem")
     norm_pairs = 2.0 * members * (members - 1)
-    regrouped = lax.all_to_all(remapped, "mem", split_axis=2, concat_axis=0, tiled=True)
+    cells = jnp.split(remapped, lax.axis_size("mem"), axis=2)
+    received = lax.all_to_all(jnp.stack(cells), "mem", 0, 0)
+    regrouped = jnp.concatenate(received, axis=0)
     part_cells = regrouped.shape[2]
     observed_part = lax.dynamic_slice_in_dim(
         observed, lax.axis_index("mem") * part_cells, part_cells, 1

time: 200 us -> 190 us (0.950)
  local copies, waits for them, and re-layouts: 40.5 us -> 34 us
  other arithmetic: 13.4 us -> 8.91 us
    all_to_all x3 -> x0, local copies, waits for them, and re-layouts: 7.94 us -> none  [on_device(): lax.all_to_all(remapped, 'mem', split_axis=2, concat_axis=0, tiled=True)]
    all_to_all x1 -> x0, other arithmetic: 4.51 us -> none  [on_device(): lax.all_to_all(remapped, 'mem', split_axis=2, concat_axis=0, tiled=True)]
    transpose x1 -> x0, local copies, waits for them, and re-layouts: 4.22 us -> none  [on_device(): remapped = summed.reshape(owned, groups, levels, block_cells).transpose(1...]
    reshape x0 -> x1, local copies, waits for them, and re-layouts: none -> 2.13 us  [on_device(): remapped = summed.reshape(owned, groups, levels, block_cells).transpose(1...]
    unnamed x8 -> x13, local copies, waits for them, and re-layouts: 13.3 us -> 15 us
where the time goes in v1:
time: 190 us; the launch traced here: 189 us
  waiting for transfers between devices  75.3 us (40%)
  starting transfers between devices  36.5 us (19%)
  local copies, waits for them, and re-layouts  34 us (18%)
  matrix products  13.4 us (7%)
  blocking collectives  11.9 us (6%)
  other arithmetic  8.91 us (5%)
  loops' own time  7.75 us (4%)
    ppermute x6, waiting for transfers between devices, from_behind(): lax.ppermute(value, axis, [(source, source + steps) for source in range(f...  52.1 us
    ppermute x6, starting transfers between devices, from_behind(): lax.ppermute(value, axis, [(source, source + steps) for source in range(f...  23.7 us
    all_to_all x1, waiting for transfers between devices, on_device(): received = lax.all_to_all(jnp.stack(cells), 'mem', 0, 0)  23.2 us
    unnamed x13, local copies, waits for them, and re-layouts  15 us
    all_to_all x1, starting transfers between devices, on_device(): received = lax.all_to_all(jnp.stack(cells), 'mem', 0, 0)  12.8 us
    all_to_all x1, blocking collectives, sent_to_all(): return lax.all_to_all(copies, axis, split_axis=0, concat_axis=0, tiled=True)  11.9 us
    dot_general x1, matrix products, on_device(): jnp.dot(chooser, partial_value.reshape(tile_slots, channels * block_cells...  10 us
    another operation x1, loops' own time, pair_total(): return lax.map(block_pairs, column_starts).reshape(left_set.shape[1:])  7.75 us
  transfers between devices with their start and end apart: 7, of which 5 were waited for; matrix products, arithmetic and copies ran while one was open for 1% of the time, Pallas kernels for 0%

profile of v1, /device:TPU:2, one launch (start us, length us, event | category | flops | bytes accessed | tf_op | source)
XLA Modules:
  0.0 188.6 jit_solution(16534641953892245516)
XLA Ops:
  0.0 0.0 copy-start
  0.0 0.0 copy-start.1
  0.0 0.8 compare_select_fusion
  0.8 0.8 compare_and_fusion
  1.6 1.7 copy.14
  3.4 1.8 copy.11
  5.8 0.0 copy-done.1
  5.9 4.9 %gather_fusion = bf16[96,192,128]{2,1,0:T(8,128)(2,1)} fusion(bf16[192,32,128]{2,0,1:T(8,128)(2,1)} %copy.11, s32[1024]{0:T(1024)S(1)} %pad_clamp_fusion), kind=kCustom, calls=%fused_computation | custom fusion | bytes 9437568 | tf_op jit(solution)/shard_map/jit(_take)/gather | solution.py:53
  10.7 0.0 copy-done
  10.7 3.4 %fusion.3 = f32[96,192,128]{2,1,0:T(8,128)S(1)} fusion(bf16[96,128,128]{2,1,0:T(8,128)(2,1)S(1)} %copy-done, bf16[96,192,128]{2,1,0:T(8,128)(2,1)} %gather_fusion, pred[96]{0:T(512)(128)(4,1)S(1)} %compare_and_fusion), kind=kOutput, calls=%fused_computation.6 | convolution fusion | flops 606339072 | bytes 17301600 | tf_op jit(solution)/shard_map/csi,sij->scj/dot_general | solution.py:54
  14.1 10.0 %fusion = f32[72,24576]{1,0:T(8,128)S(1)} fusion(f32[12,8,192,128]{3,2,1,0:T(8,128)S(1)} %bitcast.93, s32[96]{0:T(128)S(1)} %broadcast_subtract_fusion, pred[96]{0:T(512)(128)(4,1)S(1)} %iota_compare_fusion.1), kind=kOutput, calls=%fused_computation.3 | convolution fusion | flops 2038445568 | bytes 16515552 | tf_op jit(solution)/shard_map/dot_general | solution.py:64
  24.2 0.4 fusion.21
  24.5 0.1 pad_maximum_fusion.1
  24.6 4.8 %collective-permute-start.1 = (f32[2,8,24576]{2,1,0:T(8,128)S(1)}, f32[2,8,24576]{2,1,0:T(8,128)S(1)}, u32[]{:S(2)}, u32[]{:S(2)}) collective-permute-start(f32[2,8,24576]{2,1,0:T(8,128)S(1)} %pad_maximum_fusion.1), channel_id=1, source_target_pairs={{8,0},{16,8},{24,16},{32,24},{40,32},{48,40},{56,48},{64,56},{72,6... | collective-permute-start | bytes 4718600 | tf_op jit(solution)/shard_map/ppermute | solution.py:13
  29.4 0.1 pad_maximum_fusion
  29.5 1.9 %collective-permute-start = (f32[2,8,24576]{2,1,0:T(8,128)S(1)}, f32[2,8,24576]{2,1,0:T(8,128)S(1)}, u32[]{:S(2)}, u32[]{:S(2)}) collective-permute-start(f32[2,8,24576]{2,1,0:T(8,128)S(1)} %pad_maximum_fusion), channel_id=1, source_target_pairs={{0,8},{8,16},{16,24},{24,32},{32,40},{40,48},{48,56},{56,64},{64,7... | collective-permute-start | bytes 4718600 | tf_op jit(solution)/shard_map/ppermute | solution.py:13
  31.5 2.1 %collective-permute-start.4 = (f32[1,8,24576]{2,1,0:T(8,128)S(1)}, f32[1,8,24576]{2,1,0:T(8,128)S(1)}, u32[]{:S(2)}, u32[]{:S(2)}) collective-permute-start(f32[1,8,24576]{2,1,0:T(8,128)S(1)} %get-tuple-element.52), channel_id=1, source_target_pairs={{0,32},{8,40},{16,48},{24,56},{32,64},{40,72},{48,80},{56,88},{64,... | collective-permute-start | bytes 2359304 | tf_op jit(solution)/shard_map/ppermute | solution.py:13
  33.6 6.9 %collective-permute-start.5 = (f32[1,8,24576]{2,1,0:T(8,128)S(1)}, f32[1,8,24576]{2,1,0:T(8,128)S(1)}, u32[]{:S(2)}, u32[]{:S(2)}) collective-permute-start(f32[1,8,24576]{2,1,0:T(8,128)S(1)} %get-tuple-element.51), channel_id=1, source_target_pairs={{32,0},{40,8},{48,16},{56,24},{64,32},{72,40},{80,48},{88,56},{96,... | collective-permute-start | bytes 2359304 | tf_op jit(solution)/shard_map/ppermute | solution.py:13
  40.5 28.0 %collective-permute-done.1 = f32[2,8,24576]{2,1,0:T(8,128)S(1)} collective-permute-done((f32[2,8,24576]{2,1,0:T(8,128)S(1)}, f32[2,8,24576]{2,1,0:T(8,128)S(1)}, u32[]{:S(2)}, u32[]{:S(2)}) %collective-permute-start.1) | collective-permute-done | bytes 1572896 | tf_op jit(solution)/shard_map/ppermute | solution.py:13
  68.5 3.9 %collective-permute-done = f32[2,8,24576]{2,1,0:T(8,128)S(1)} collective-permute-done((f32[2,8,24576]{2,1,0:T(8,128)S(1)}, f32[2,8,24576]{2,1,0:T(8,128)S(1)}, u32[]{:S(2)}, u32[]{:S(2)}) %collective-permute-start) | collective-permute-done | bytes 1572896 | tf_op jit(solution)/shard_map/ppermute | solution.py:13
  72.4 0.3 slice_add_fusion.1
  72.7 1.9 %collective-permute-start.2 = (f32[1,8,24576]{2,1,0:T(8,128)S(1)}, f32[1,8,24576]{2,1,0:T(8,128)S(1)}, u32[]{:S(2)}, u32[]{:S(2)}) collective-permute-start(f32[1,8,24576]{2,1,0:T(8,128)S(1)} %get-tuple-element.57), channel_id=1, source_target_pairs={{0,16},{8,24},{16,32},{24,40},{32,48},{40,56},{48,64},{56,72},{64,... | collective-permute-start | bytes 2359304 | tf_op jit(solution)/shard_map/ppermute | solution.py:13
  74.6 6.0 %collective-permute-start.3 = (f32[1,8,24576]{2,1,0:T(8,128)S(1)}, f32[1,8,24576]{2,1,0:T(8,128)S(1)}, u32[]{:S(2)}, u32[]{:S(2)}) collective-permute-start(f32[1,8,24576]{2,1,0:T(8,128)S(1)} %get-tuple-element.58), channel_id=1, source_target_pairs={{16,0},{24,8},{32,16},{40,24},{48,32},{56,40},{64,48},{72,56},{80,... | collective-permute-start | bytes 2359304 | tf_op jit(solution)/shard_map/ppermute | solution.py:13
  80.6 0.0 collective-permute-done.4
  80.6 1.7 collective-permute-done.5
  82.4 18.5 %collective-permute-done.2 = f32[1,8,24576]{2,1,0:T(8,128)S(1)} collective-permute-done((f32[1,8,24576]{2,1,0:T(8,128)S(1)}, f32[1,8,24576]{2,1,0:T(8,128)S(1)}, u32[]{:S(2)}, u32[]{:S(2)}) %collective-permute-start.2) | collective-permute-done | bytes 786464 | tf_op jit(solution)/shard_map/ppermute | solution.py:13
  100.9 0.0 collective-permute-done.3
  100.9 1.2 add_bitcast_fusion
  102.1 2.1 %reshape.54 = f32[6,32,1024]{2,1,0:T(8,128)} reshape(f32[6,32,8,128]{3,2,1,0:T(8,128)} %add_bitcast_fusion) | data formatting | bytes 1572864 | tf_op jit(solution)/shard_map/reshape | solution.py:96
  104.3 1.5 fusion.15
  105.8 1.5 fusion.14
  107.3 1.5 fusion.13
  108.9 1.5 fusion.12
  110.4 1.5 fusion.11
  111.9 1.5 fusion.10
  113.5 1.5 fusion.9
  115.0 1.5 fusion.8
  116.5 12.8 %all-to-all-start = ((f32[8,6,32,128]{3,2,1,0:T(8,128)}), f32[8,6,32,128]{3,2,1,0:T(8,128)}, u32[]{:S(2)}, u32[]{:S(2)}) async-start(f32[8,6,32,128]{3,2,1,0:T(8,128)} %fusion.8), calls=%async_computation | async-start | bytes 1572864 | tf_op jit(solution)/shard_map/all_to_all | solution.py:101
  129.3 0.7 constant_dynamic-slice_fusion.1
  130.0 23.2 %all-to-all-done = f32[8,6,32,128]{3,2,1,0:T(8,128)} async-done(((f32[8,6,32,128]{3,2,1,0:T(8,128)}), f32[8,6,32,128]{3,2,1,0:T(8,128)}, u32[]{:S(2)}, u32[]{:S(2)}) %all-to-all-start) | async-done | bytes 786464 | tf_op jit(solution)/shard_map/all_to_all | solution.py:101
  153.2 2.5 %copy.23 = f32[6,8,32,128]{3,1,2,0:T(8,128)} copy(f32[6,8,32,128]{3,2,1,0:T(8,128)} %bitcast.38) | data formatting | bytes 1572864
  155.7 19.0 %while.11 = (s32[]{:T(128)}, f32[4,1024]{1,0:T(4,128)S(1)}, s32[4]{0:T(128)S(1)}, f32[48,4096]{1,0:T(8,128)}, s32[]{:T(128)}, /*index=5*/s32[]{:T(128)}, s32[]{:T(128)}) while((s32[]{:T(128)}, f32[4,1024]{1,0:T(4,128)S(1)}, s32[4]{0:T(128)S(1)}, f32[48,4096]{1,0:T(8,128)}, s32[]{:T(128)}, /*index=5*/s32[]{:T(128)}, s32[]{:T(128)}) %tuple.33), condition=%wide.region_3.4_spmd, body=%wide.region_1.3_spmd.sunk | while | flops 7076869 | bytes 602243 | solution.py:44
  155.7 0.6 dynamic_slice.20
  158.2 1.1 constant_dynamic-slice_fusion.3
  159.3 1.1 abs_reduce_fusion.3
  160.3 0.1 dynamic_update_slice.6
  160.4 0.6 dynamic_slice.20
  163.0 1.1 constant_dynamic-slice_fusion.3
  164.0 1.1 abs_reduce_fusion.3
  165.1 0.1 dynamic_update_slice.6
  165.2 0.6 dynamic_slice.20
  167.7 1.1 constant_dynamic-slice_fusion.3
  168.8 1.1 abs_reduce_fusion.3
  169.8 0.1 dynamic_update_slice.6
  169.9 0.6 dynamic_slice.20
  172.5 1.0 constant_dynamic-slice_fusion.3
  173.5 1.1 abs_reduce_fusion.3
  174.6 0.1 dynamic_update_slice.6
  174.7 1.2 abs_reduce_fusion.1
  176.0 11.9 %all_to_all.10 = f32[8,32,128]{2,1,0:T(8,128)S(1)} all-to-all(f32[8,32,128]{2,1,0:T(8,128)S(1)} %broadcast_in_dim.35), channel_id=1, replica_groups=mesh['dom'=64,'mem'=8] {'mem'}, dimensions={0} | all-to-all | bytes 262144 | tf_op jit(solution)/shard_map/all_to_all | solution.py:18
  187.9 0.7 copy_bitcast_fusion.1
  (9 shorter events, 0.1 us)
Async XLA Ops:
  0.0 10.7 %copy-start = (bf16[96,128,128]{2,1,0:T(8,128)(2,1)S(1)}, bf16[96,128,128]{2,1,0:T(8,128)(2,1)}, u32[]{:S(2)}) copy-start(bf16[96,128,128]{2,1,0:T(8,128)(2,1)} %param.10) | copy-start | bytes 9437188
  0.0 5.8 %copy-start.1 = (s32[96]{0:T(128)S(1)}, s32[96]{0:T(128)}, u32[]{:S(2)}) copy-start(s32[96]{0:T(128)} %param.12) | copy-start | bytes 1156
  24.6 43.9 %collective-permute-start.1 = (f32[2,8,24576]{2,1,0:T(8,128)S(1)}, f32[2,8,24576]{2,1,0:T(8,128)S(1)}, u32[]{:S(2)}, u32[]{:S(2)}) collective-permute-start(f32[2,8,24576]{2,1,0:T(8,128)S(1)} %pad_maximum_fusion.1), channel_id=1, source_target_pairs={{8,0},{16,8},{24,16},{32,24},{40,32},{48,40},{56,48},{64,56},{72,6... | collective-permute-start | bytes 4718600 | tf_op jit(solution)/shard_map/ppermute | solution.py:13
  29.5 42.9 %collective-permute-start = (f32[2,8,24576]{2,1,0:T(8,128)S(1)}, f32[2,8,24576]{2,1,0:T(8,128)S(1)}, u32[]{:S(2)}, u32[]{:S(2)}) collective-permute-start(f32[2,8,24576]{2,1,0:T(8,128)S(1)} %pad_maximum_fusion), channel_id=1, source_target_pairs={{0,8},{8,16},{16,24},{24,32},{32,40},{40,48},{48,56},{56,64},{64,7... | collective-permute-start | bytes 4718600 | tf_op jit(solution)/shard_map/ppermute | solution.py:13
  31.5 49.2 %collective-permute-start.4 = (f32[1,8,24576]{2,1,0:T(8,128)S(1)}, f32[1,8,24576]{2,1,0:T(8,128)S(1)}, u32[]{:S(2)}, u32[]{:S(2)}) collective-permute-start(f32[1,8,24576]{2,1,0:T(8,128)S(1)} %get-tuple-element.52), channel_id=1, source_target_pairs={{0,32},{8,40},{16,48},{24,56},{32,64},{40,72},{48,80},{56,88},{64,... | collective-permute-start | bytes 2359304 | tf_op jit(solution)/shard_map/ppermute | solution.py:13
  33.6 48.8 %collective-permute-start.5 = (f32[1,8,24576]{2,1,0:T(8,128)S(1)}, f32[1,8,24576]{2,1,0:T(8,128)S(1)}, u32[]{:S(2)}, u32[]{:S(2)}) collective-permute-start(f32[1,8,24576]{2,1,0:T(8,128)S(1)} %get-tuple-element.51), channel_id=1, source_target_pairs={{32,0},{40,8},{48,16},{56,24},{64,32},{72,40},{80,48},{88,56},{96,... | collective-permute-start | bytes 2359304 | tf_op jit(solution)/shard_map/ppermute | solution.py:13
  72.7 28.2 %collective-permute-start.2 = (f32[1,8,24576]{2,1,0:T(8,128)S(1)}, f32[1,8,24576]{2,1,0:T(8,128)S(1)}, u32[]{:S(2)}, u32[]{:S(2)}) collective-permute-start(f32[1,8,24576]{2,1,0:T(8,128)S(1)} %get-tuple-element.57), channel_id=1, source_target_pairs={{0,16},{8,24},{16,32},{24,40},{32,48},{40,56},{48,64},{56,72},{64,... | collective-permute-start | bytes 2359304 | tf_op jit(solution)/shard_map/ppermute | solution.py:13
  74.6 26.3 %collective-permute-start.3 = (f32[1,8,24576]{2,1,0:T(8,128)S(1)}, f32[1,8,24576]{2,1,0:T(8,128)S(1)}, u32[]{:S(2)}, u32[]{:S(2)}) collective-permute-start(f32[1,8,24576]{2,1,0:T(8,128)S(1)} %get-tuple-element.58), channel_id=1, source_target_pairs={{16,0},{24,8},{32,16},{40,24},{48,32},{56,40},{64,48},{72,56},{80,... | collective-permute-start | bytes 2359304 | tf_op jit(solution)/shard_map/ppermute | solution.py:13
  116.5 36.7 %all-to-all-start = ((f32[8,6,32,128]{3,2,1,0:T(8,128)}), f32[8,6,32,128]{3,2,1,0:T(8,128)}, u32[]{:S(2)}, u32[]{:S(2)}) async-start(f32[8,6,32,128]{3,2,1,0:T(8,128)} %fusion.8), calls=%async_computation | async-start | bytes 1572864 | tf_op jit(solution)/shard_map/all_to_all | solution.py:101
